TPU v7x, 32 devices: a whole 2x2x4 slice. The times are simulated.
32 devices in a mesh: data: 2 (over x), cp: 16 (over z, y, core).
Axes of the slice: x: 2, y: 2, z: 4, core: 2. Of those that a mesh axis runs over, the one named last changes fastest.
Arguments:
- q: bfloat16 [16384, 8, 128], P(('data', 'cp')), parts along dimension 0
- k: bfloat16 [16384, 8, 128], P(('data', 'cp')), parts along dimension 0
- v: bfloat16 [16384, 8, 128], P(('data', 'cp')), parts along dimension 0
- o: bfloat16 [16384, 8, 128], P(('data', 'cp')), parts along dimension 0
- dout: bfloat16 [16384, 8, 128], P(('data', 'cp')), parts along dimension 0
- lse: float32 [8, 16384], P(None, ('data', 'cp')), parts along dimension 1
Outputs:
- output 1: bfloat16 [16384, 8, 128], P(('data', 'cp')), parts along dimension 0
- output 2: bfloat16 [16384, 8, 128], P(('data', 'cp')), parts along dimension 0
- output 3: bfloat16 [16384, 8, 128], P(('data', 'cp')), parts along dimension 0
There are 2 independent parts. A program takes and returns all parts, laid end to end along the dimension named above; each array names one.
All inputs are finite; a program needn't handle non-finite values.
Results may differ from a plain program's by a relative error of at most 0.001.
Values are sent between devices in bfloat16 or wider.
A program may use at most 1 GiB of HBM per device.

v0:
```python
import jax
import jax.numpy as jnp
from jax import lax
from jax.sharding import PartitionSpec as P

TILE = 512


def _tiles(q, dout, o, lse, n, me):
    c, h, d = q.shape
    m = c // TILE
    dd = jnp.einsum('qhd,qhd->hq', dout, o, preferred_element_type=jnp.float32)
    qpos = jnp.arange(c, dtype=jnp.int32) * n + me
    return (q.reshape(m, TILE, h, d), dout.reshape(m, TILE, h, d),
            lse.reshape(h, m, TILE).transpose(1, 0, 2),
            dd.reshape(h, m, TILE).transpose(1, 0, 2),
            qpos.reshape(m, TILE))


def _block_grads(xs, kb, vb, kpos, gk, gv, scale):
    f32 = jnp.float32

    def body(carry, x):
        gk, gv = carry
        qt, dt, lt, et, pt = x
        s = jnp.einsum('qhd,khd->hqk', qt, kb, preferred_element_type=f32) * scale
        mask = kpos[None, :] <= pt[:, None]
        p = jnp.where(mask[None], jnp.exp(s - lt[:, :, None]), 0.0)
        gv = gv + jnp.einsum('hqk,qhd->khd', p.astype(jnp.bfloat16), dt, preferred_element_type=f32)
        dp = jnp.einsum('qhd,khd->hqk', dt, vb, preferred_element_type=f32)
        ds = (p * (dp - et[:, :, None])).astype(jnp.bfloat16)
        dq = jnp.einsum('hqk,khd->qhd', ds, kb, preferred_element_type=f32) * scale
        gk = gk + jnp.einsum('hqk,qhd->khd', ds, qt, preferred_element_type=f32) * scale
        return (gk, gv), dq

    (gk, gv), dq = lax.scan(body, (gk, gv), xs)
    return dq, gk, gv


def solution(mesh):
    n = mesh.shape['cp']
    rows = P(('data', 'cp'))
    cols = P(None, ('data', 'cp'))
    perm = [(i, (i + 1) % n) for i in range(n)]

    def local(q, k, v, o, dout, lse):
        c, h, d = q.shape
        scale = d ** -0.5
        me = lax.axis_index('cp')
        xs = _tiles(q, dout, o, lse, n, me)
        base = jnp.arange(c, dtype=jnp.int32) * n
        dq = jnp.zeros((c // TILE, TILE, h, d), jnp.float32)
        gk = jnp.zeros((c, h, d), jnp.float32)
        gv = jnp.zeros((c, h, d), jnp.float32)
        kb, vb = k, v
        for s in range(n):
            kpos = base + (me - s) % n
            dqs, gk, gv = _block_grads(xs, kb, vb, kpos, gk, gv, scale)
            dq = dq + dqs
            if s < n - 1:
                kb = lax.ppermute(kb, 'cp', perm)
                vb = lax.ppermute(vb, 'cp', perm)
            gk = lax.ppermute(gk, 'cp', perm)
            gv = lax.ppermute(gv, 'cp', perm)
        return (dq.reshape(c, h, d).astype(jnp.bfloat16),
                gk.astype(jnp.bfloat16), gv.astype(jnp.bfloat16))

    return jax.shard_map(local, mesh=mesh, in_specs=(rows, rows, rows, rows, rows, cols),
                         out_specs=(rows, rows, rows), check_vma=False)
```

profile of v0, /device:TPU:0, one launch (start us, length us, event | category | flops | bytes accessed | tf_op | source)
XLA Modules:
  0.0 1049.5 jit_solution(3039310458703858184)
XLA Ops:
  58.1 30.7 %collective-permute-done.2 = bf16[512,8,128]{2,0,1:T(8,128)(2,1)S(1)} collective-permute-done((bf16[512,8,128]{2,0,1:T(8,128)(2,1)S(1)}, bf16[512,8,128]{2,0,1:T(8,128)(2,1)S(1)}, u32[]{:S(2)}, u32[]{:S(2)}) %collective-permute-start.2) | collective-permute-done | bytes 1048608 | tf_op jit(solution)/shard_map/ppermute | solution.py:61
  159.4 19.2 %collective-permute-done.6 = bf16[512,8,128]{2,0,1:T(8,128)(2,1)S(1)} collective-permute-done((bf16[512,8,128]{2,0,1:T(8,128)(2,1)S(1)}, bf16[512,8,128]{2,0,1:T(8,128)(2,1)S(1)}, u32[]{:S(2)}, u32[]{:S(2)}) %collective-permute-start.6) | collective-permute-done | bytes 1048608 | tf_op jit(solution)/shard_map/ppermute | solution.py:61
  206.2 17.4 %collective-permute-done.8 = bf16[512,8,128]{2,0,1:T(8,128)(2,1)S(1)} collective-permute-done((bf16[512,8,128]{2,0,1:T(8,128)(2,1)S(1)}, bf16[512,8,128]{2,0,1:T(8,128)(2,1)S(1)}, u32[]{:S(2)}, u32[]{:S(2)}) %collective-permute-start.8) | collective-permute-done | bytes 1048608 | tf_op jit(solution)/shard_map/ppermute | solution.py:61
  288.4 47.5 %collective-permute-done.12 = bf16[512,8,128]{2,0,1:T(8,128)(2,1)S(1)} collective-permute-done((bf16[512,8,128]{2,0,1:T(8,128)(2,1)S(1)}, bf16[512,8,128]{2,0,1:T(8,128)(2,1)S(1)}, u32[]{:S(2)}, u32[]{:S(2)}) %collective-permute-start.12) | collective-permute-done | bytes 1048608 | tf_op jit(solution)/shard_map/ppermute | solution.py:61
  387.3 40.9 %collective-permute-done.16 = bf16[512,8,128]{2,0,1:T(8,128)(2,1)S(1)} collective-permute-done((bf16[512,8,128]{2,0,1:T(8,128)(2,1)S(1)}, bf16[512,8,128]{2,0,1:T(8,128)(2,1)S(1)}, u32[]{:S(2)}, u32[]{:S(2)}) %collective-permute-start.16) | collective-permute-done | bytes 1048608 | tf_op jit(solution)/shard_map/ppermute | solution.py:61
  465.2 19.2 %collective-permute-done.35 = f32[512,8,128]{2,0,1:T(8,128)S(1)} collective-permute-done((f32[512,8,128]{2,0,1:T(8,128)S(1)}, f32[512,8,128]{2,0,1:T(8,128)S(1)}, u32[]{:S(2)}, u32[]{:S(2)}) %collective-permute-start.35) | collective-permute-done | bytes 2097184 | tf_op jit(solution)/shard_map/ppermute | solution.py:63
  486.0 20.8 %collective-permute-done.51 = f32[512,8,128]{2,0,1:T(8,128)S(1)} collective-permute-done((f32[512,8,128]{2,0,1:T(8,128)}, f32[512,8,128]{2,0,1:T(8,128)S(1)}, u32[]{:S(2)}, u32[]{:S(2)}) %collective-permute-start.51) | collective-permute-done | bytes 2097184 | tf_op jit(solution)/shard_map/ppermute | solution.py:64
  516.2 13.1 %collective-permute-done.36 = f32[512,8,128]{2,0,1:T(8,128)} collective-permute-done((f32[512,8,128]{2,0,1:T(8,128)}, f32[512,8,128]{2,0,1:T(8,128)}, u32[]{:S(2)}, u32[]{:S(2)}) %collective-permute-start.36) | collective-permute-done | bytes 2097184 | tf_op jit(solution)/shard_map/ppermute | solution.py:63
  531.3 20.5 %collective-permute-done.52 = f32[512,8,128]{2,0,1:T(8,128)} collective-permute-done((f32[512,8,128]{2,0,1:T(8,128)}, f32[512,8,128]{2,0,1:T(8,128)}, u32[]{:S(2)}, u32[]{:S(2)}) %collective-permute-start.52) | collective-permute-done | bytes 2097184 | tf_op jit(solution)/shard_map/ppermute | solution.py:64
  575.6 21.2 %collective-permute-done.37 = f32[512,8,128]{2,0,1:T(8,128)S(1)} collective-permute-done((f32[512,8,128]{2,0,1:T(8,128)S(1)}, f32[512,8,128]{2,0,1:T(8,128)S(1)}, u32[]{:S(2)}, u32[]{:S(2)}) %collective-permute-start.37) | collective-permute-done | bytes 2097184 | tf_op jit(solution)/shard_map/ppermute | solution.py:63
  598.3 20.9 %collective-permute-done.53 = f32[512,8,128]{2,0,1:T(8,128)} collective-permute-done((f32[512,8,128]{2,0,1:T(8,128)}, f32[512,8,128]{2,0,1:T(8,128)}, u32[]{:S(2)}, u32[]{:S(2)}) %collective-permute-start.53) | collective-permute-done | bytes 2097184 | tf_op jit(solution)/shard_map/ppermute | solution.py:64
  634.2 30.0 %collective-permute-done.38 = f32[512,8,128]{2,0,1:T(8,128)} collective-permute-done((f32[512,8,128]{2,0,1:T(8,128)}, f32[512,8,128]{2,0,1:T(8,128)}, u32[]{:S(2)}, u32[]{:S(2)}) %collective-permute-start.38) | collective-permute-done | bytes 2097184 | tf_op jit(solution)/shard_map/ppermute | solution.py:63
  666.1 20.5 %collective-permute-done.54 = f32[512,8,128]{2,0,1:T(8,128)} collective-permute-done((f32[512,8,128]{2,0,1:T(8,128)}, f32[512,8,128]{2,0,1:T(8,128)}, u32[]{:S(2)}, u32[]{:S(2)}) %collective-permute-start.54) | collective-permute-done | bytes 2097184 | tf_op jit(solution)/shard_map/ppermute | solution.py:64
  711.1 20.5 %collective-permute-done.55 = f32[512,8,128]{2,0,1:T(8,128)} collective-permute-done((f32[512,8,128]{2,0,1:T(8,128)}, f32[512,8,128]{2,0,1:T(8,128)}, u32[]{:S(2)}, u32[]{:S(2)}) %collective-permute-start.55) | collective-permute-done | bytes 2097184 | tf_op jit(solution)/shard_map/ppermute | solution.py:64
  755.3 21.2 %collective-permute-done.40 = f32[512,8,128]{2,0,1:T(8,128)S(1)} collective-permute-done((f32[512,8,128]{2,0,1:T(8,128)S(1)}, f32[512,8,128]{2,0,1:T(8,128)S(1)}, u32[]{:S(2)}, u32[]{:S(2)}) %collective-permute-start.40) | collective-permute-done | bytes 2097184 | tf_op jit(solution)/shard_map/ppermute | solution.py:63
  778.1 20.9 %collective-permute-done.56 = f32[512,8,128]{2,0,1:T(8,128)} collective-permute-done((f32[512,8,128]{2,0,1:T(8,128)}, f32[512,8,128]{2,0,1:T(8,128)}, u32[]{:S(2)}, u32[]{:S(2)}) %collective-permute-start.56) | collective-permute-done | bytes 2097184 | tf_op jit(solution)/shard_map/ppermute | solution.py:64
  812.4 31.5 %collective-permute-done.41 = f32[512,8,128]{2,0,1:T(8,128)} collective-permute-done((f32[512,8,128]{2,0,1:T(8,128)}, f32[512,8,128]{2,0,1:T(8,128)}, u32[]{:S(2)}, u32[]{:S(2)}) %collective-permute-start.41) | collective-permute-done | bytes 2097184 | tf_op jit(solution)/shard_map/ppermute | solution.py:63
  845.9 20.5 %collective-permute-done.57 = f32[512,8,128]{2,0,1:T(8,128)} collective-permute-done((f32[512,8,128]{2,0,1:T(8,128)}, f32[512,8,128]{2,0,1:T(8,128)}, u32[]{:S(2)}, u32[]{:S(2)}) %collective-permute-start.57) | collective-permute-done | bytes 2097184 | tf_op jit(solution)/shard_map/ppermute | solution.py:64
  876.2 12.7 %collective-permute-done.42 = f32[512,8,128]{2,0,1:T(8,128)} collective-permute-done((f32[512,8,128]{2,0,1:T(8,128)S(1)}, f32[512,8,128]{2,0,1:T(8,128)}, u32[]{:S(2)}, u32[]{:S(2)}) %collective-permute-start.42) | collective-permute-done | bytes 2097184 | tf_op jit(solution)/shard_map/ppermute | solution.py:63
  890.8 20.5 %collective-permute-done.58 = f32[512,8,128]{2,0,1:T(8,128)} collective-permute-done((f32[512,8,128]{2,0,1:T(8,128)S(1)}, f32[512,8,128]{2,0,1:T(8,128)}, u32[]{:S(2)}, u32[]{:S(2)}) %collective-permute-start.58) | collective-permute-done | bytes 2097184 | tf_op jit(solution)/shard_map/ppermute | solution.py:64
  923.9 32.4 %collective-permute-done.43 = f32[512,8,128]{2,0,1:T(8,128)S(1)} collective-permute-done((f32[512,8,128]{2,0,1:T(8,128)S(1)}, f32[512,8,128]{2,0,1:T(8,128)S(1)}, u32[]{:S(2)}, u32[]{:S(2)}) %collective-permute-start.43) | collective-permute-done | bytes 2097184 | tf_op jit(solution)/shard_map/ppermute | solution.py:63
  956.7 22.0 %collective-permute-done.59 = f32[512,8,128]{2,0,1:T(8,128)S(1)} collective-permute-done((f32[512,8,128]{2,0,1:T(8,128)S(1)}, f32[512,8,128]{2,0,1:T(8,128)S(1)}, u32[]{:S(2)}, u32[]{:S(2)}) %collective-permute-start.59) | collective-permute-done | bytes 2097184 | tf_op jit(solution)/shard_map/ppermute | solution.py:64
  1004.2 19.5 %collective-permute-done.60 = f32[512,8,128]{2,0,1:T(8,128)} collective-permute-done((f32[512,8,128]{2,0,1:T(8,128)}, f32[512,8,128]{2,0,1:T(8,128)}, u32[]{:S(2)}, u32[]{:S(2)}) %collective-permute-start.60) | collective-permute-done | bytes 2097184 | tf_op jit(solution)/shard_map/ppermute | solution.py:64
  1027.1 12.3 %bitcast_convert_fusion = bf16[512,8,128]{2,0,1:T(8,128)(2,1)} fusion(f32[8,512,128]{2,1,0:T(8,128)} %fusion.278, f32[8,512,128]{2,1,0:T(8,128)} %fusion.277, f32[8,512,128]{2,1,0:T(8,128)} %fusion.276, f32[8,512,128]{2,1,0:T(8,128)} %fusion.275, f32[8,512,128]{2,1,0:T(8,128)} %fusion.274, f32[8,512,128]{2,1,0:T(8,128)} %fusion.273, ...), kind=kOutput, calls=%fused_computation.158 | convolution fusion | flops 545783808 | bytes 37748736 | tf_op jit(solution)/shard_map/while/body/eval_jaxpr/hqk,khd->qhd/dot_general | solution.py:32
  (314 shorter events, 491.3 us)
Async XLA Ops:
  31.1 80.3 %collective-permute-start.46 = (f32[512,8,128]{2,0,1:T(8,128)}, f32[512,8,128]{2,0,1:T(8,128)S(1)}, u32[]{:S(2)}, u32[]{:S(2)}) collective-permute-start(f32[512,8,128]{2,0,1:T(8,128)} %fusion.113), channel_id=1, source_target_pairs={{0,1},{1,2},{2,3},{3,4},{4,5},{5,6},{6,7},{7,8},{8,9},{9,10},{10,1... | collective-permute-start | bytes 6291464 | tf_op jit(solution)/shard_map/ppermute | solution.py:64
  58.1 99.8 %collective-permute-start.31 = (f32[512,8,128]{2,0,1:T(8,128)}, f32[512,8,128]{2,0,1:T(8,128)S(1)}, u32[]{:S(2)}, u32[]{:S(2)}) collective-permute-start(f32[512,8,128]{2,0,1:T(8,128)} %bitcast_add_fusion.29), channel_id=1, source_target_pairs={{0,1},{1,2},{2,3},{3,4},{4,5},{5,6},{6,7},{7,8},{8,9},{9,10},{10,1... | collective-permute-start | bytes 6291464 | tf_op jit(solution)/shard_map/ppermute | solution.py:63
  118.6 81.8 %collective-permute-start.47 = (f32[512,8,128]{2,0,1:T(8,128)}, f32[512,8,128]{2,0,1:T(8,128)}, u32[]{:S(2)}, u32[]{:S(2)}) collective-permute-start(f32[512,8,128]{2,0,1:T(8,128)} %bitcast_add_fusion.14), channel_id=1, source_target_pairs={{0,1},{1,2},{2,3},{3,4},{4,5},{5,6},{6,7},{7,8},{8,9},{9,10},{10,1... | collective-permute-start | bytes 6291464 | tf_op jit(solution)/shard_map/ppermute | solution.py:64
  159.4 88.3 %collective-permute-start.32 = (f32[512,8,128]{2,0,1:T(8,128)}, f32[512,8,128]{2,0,1:T(8,128)}, u32[]{:S(2)}, u32[]{:S(2)}) collective-permute-start(f32[512,8,128]{2,0,1:T(8,128)} %bitcast_add_fusion.28), channel_id=1, source_target_pairs={{0,1},{1,2},{2,3},{3,4},{4,5},{5,6},{6,7},{7,8},{8,9},{9,10},{10,1... | collective-permute-start | bytes 6291464 | tf_op jit(solution)/shard_map/ppermute | solution.py:63
  251.1 113.1 %collective-permute-start.33 = (f32[512,8,128]{2,0,1:T(8,128)}, f32[512,8,128]{2,0,1:T(8,128)}, u32[]{:S(2)}, u32[]{:S(2)}) collective-permute-start(f32[512,8,128]{2,0,1:T(8,128)} %bitcast_add_fusion.27), channel_id=1, source_target_pairs={{0,1},{1,2},{2,3},{3,4},{4,5},{5,6},{6,7},{7,8},{8,9},{9,10},{10,1... | collective-permute-start | bytes 6291464 | tf_op jit(solution)/shard_map/ppermute | solution.py:63
  260.5 105.8 %collective-permute-start.49 = (f32[512,8,128]{2,0,1:T(8,128)}, f32[512,8,128]{2,0,1:T(8,128)}, u32[]{:S(2)}, u32[]{:S(2)}) collective-permute-start(f32[512,8,128]{2,0,1:T(8,128)} %bitcast_add_fusion.12), channel_id=1, source_target_pairs={{0,1},{1,2},{2,3},{3,4},{4,5},{5,6},{6,7},{7,8},{8,9},{9,10},{10,1... | collective-permute-start | bytes 6291464 | tf_op jit(solution)/shard_map/ppermute | solution.py:64
  268.5 67.4 %collective-permute-start.12 = (bf16[512,8,128]{2,0,1:T(8,128)(2,1)S(1)}, bf16[512,8,128]{2,0,1:T(8,128)(2,1)S(1)}, u32[]{:S(2)}, u32[]{:S(2)}) collective-permute-start(bf16[512,8,128]{2,0,1:T(8,128)(2,1)S(1)} %collective-permute-done.10), channel_id=1, source_target_pairs={{0,1},{1,2},{2,3},{3,4},{4,5},{5,6},{6,7},{7,8},{8,9},{9,10},{10,1... | collective-permute-start | bytes 3145736 | tf_op jit(solution)/shard_map/ppermute | solution.py:61
  279.7 67.4 %collective-permute-start.13 = (bf16[512,8,128]{2,0,1:T(8,128)(2,1)}, bf16[512,8,128]{2,0,1:T(8,128)(2,1)}, u32[]{:S(2)}, u32[]{:S(2)}) collective-permute-start(bf16[512,8,128]{2,0,1:T(8,128)(2,1)} %collective-permute-done.11), channel_id=1, source_target_pairs={{0,1},{1,2},{2,3},{3,4},{4,5},{5,6},{6,7},{7,8},{8,9},{9,10},{10,1... | collective-permute-start | bytes 3145736 | tf_op jit(solution)/shard_map/ppermute | solution.py:62
  366.3 77.8 %collective-permute-start.34 = (f32[512,8,128]{2,0,1:T(8,128)S(1)}, f32[512,8,128]{2,0,1:T(8,128)}, u32[]{:S(2)}, u32[]{:S(2)}) collective-permute-start(f32[512,8,128]{2,0,1:T(8,128)S(1)} %bitcast_add_fusion.26), channel_id=1, source_target_pairs={{0,1},{1,2},{2,3},{3,4},{4,5},{5,6},{6,7},{7,8},{8,9},{9,10},{10,1... | collective-permute-start | bytes 6291464 | tf_op jit(solution)/shard_map/ppermute | solution.py:63
  369.7 76.5 %collective-permute-start.50 = (f32[512,8,128]{2,0,1:T(8,128)}, f32[512,8,128]{2,0,1:T(8,128)}, u32[]{:S(2)}, u32[]{:S(2)}) collective-permute-start(f32[512,8,128]{2,0,1:T(8,128)} %bitcast_add_fusion.11), channel_id=1, source_target_pairs={{0,1},{1,2},{2,3},{3,4},{4,5},{5,6},{6,7},{7,8},{8,9},{9,10},{10,1... | collective-permute-start | bytes 6291464 | tf_op jit(solution)/shard_map/ppermute | solution.py:64
  372.6 66.8 %collective-permute-start.17 = (bf16[512,8,128]{2,0,1:T(8,128)(2,1)S(1)}, bf16[512,8,128]{2,0,1:T(8,128)(2,1)}, u32[]{:S(2)}, u32[]{:S(2)}) collective-permute-start(bf16[512,8,128]{2,0,1:T(8,128)(2,1)S(1)} %collective-permute-done.15), channel_id=1, source_target_pairs={{0,1},{1,2},{2,3},{3,4},{4,5},{5,6},{6,7},{7,8},{8,9},{9,10},{10,1... | collective-permute-start | bytes 3145736 | tf_op jit(solution)/shard_map/ppermute | solution.py:62
  428.2 81.9 %collective-permute-start.18 = (bf16[512,8,128]{2,0,1:T(8,128)(2,1)S(1)}, bf16[512,8,128]{2,0,1:T(8,128)(2,1)S(1)}, u32[]{:S(2)}, u32[]{:S(2)}) collective-permute-start(bf16[512,8,128]{2,0,1:T(8,128)(2,1)S(1)} %collective-permute-done.16), channel_id=1, source_target_pairs={{0,1},{1,2},{2,3},{3,4},{4,5},{5,6},{6,7},{7,8},{8,9},{9,10},{10,1... | collective-permute-start | bytes 3145736 | tf_op jit(solution)/shard_map/ppermute | solution.py:61
  439.5 70.8 %collective-permute-start.19 = (bf16[512,8,128]{2,0,1:T(8,128)(2,1)}, bf16[512,8,128]{2,0,1:T(8,128)(2,1)}, u32[]{:S(2)}, u32[]{:S(2)}) collective-permute-start(bf16[512,8,128]{2,0,1:T(8,128)(2,1)} %collective-permute-done.17), channel_id=1, source_target_pairs={{0,1},{1,2},{2,3},{3,4},{4,5},{5,6},{6,7},{7,8},{8,9},{9,10},{10,1... | collective-permute-start | bytes 3145736 | tf_op jit(solution)/shard_map/ppermute | solution.py:62
  531.3 65.5 %collective-permute-start.37 = (f32[512,8,128]{2,0,1:T(8,128)S(1)}, f32[512,8,128]{2,0,1:T(8,128)S(1)}, u32[]{:S(2)}, u32[]{:S(2)}) collective-permute-start(f32[512,8,128]{2,0,1:T(8,128)S(1)} %bitcast_add_fusion.23), channel_id=1, source_target_pairs={{0,1},{1,2},{2,3},{3,4},{4,5},{5,6},{6,7},{7,8},{8,9},{9,10},{10,1... | collective-permute-start | bytes 6291464 | tf_op jit(solution)/shard_map/ppermute | solution.py:63
  563.4 128.0 %collective-permute-start.22 = (bf16[512,8,128]{2,0,1:T(8,128)(2,1)S(1)}, bf16[512,8,128]{2,0,1:T(8,128)(2,1)S(1)}, u32[]{:S(2)}, u32[]{:S(2)}) collective-permute-start(bf16[512,8,128]{2,0,1:T(8,128)(2,1)S(1)} %collective-permute-done.20), channel_id=1, source_target_pairs={{0,1},{1,2},{2,3},{3,4},{4,5},{5,6},{6,7},{7,8},{8,9},{9,10},{10,1... | collective-permute-start | bytes 3145736 | tf_op jit(solution)/shard_map/ppermute | solution.py:61
  574.3 117.2 %collective-permute-start.23 = (bf16[512,8,128]{2,0,1:T(8,128)(2,1)}, bf16[512,8,128]{2,0,1:T(8,128)(2,1)}, u32[]{:S(2)}, u32[]{:S(2)}) collective-permute-start(bf16[512,8,128]{2,0,1:T(8,128)(2,1)} %collective-permute-done.21), channel_id=1, source_target_pairs={{0,1},{1,2},{2,3},{3,4},{4,5},{5,6},{6,7},{7,8},{8,9},{9,10},{10,1... | collective-permute-start | bytes 3145736 | tf_op jit(solution)/shard_map/ppermute | solution.py:62
  598.3 65.9 %collective-permute-start.38 = (f32[512,8,128]{2,0,1:T(8,128)}, f32[512,8,128]{2,0,1:T(8,128)}, u32[]{:S(2)}, u32[]{:S(2)}) collective-permute-start(f32[512,8,128]{2,0,1:T(8,128)} %bitcast_add_fusion.22), channel_id=1, source_target_pairs={{0,1},{1,2},{2,3},{3,4},{4,5},{5,6},{6,7},{7,8},{8,9},{9,10},{10,1... | collective-permute-start | bytes 6291464 | tf_op jit(solution)/shard_map/ppermute | solution.py:63
  711.0 65.5 %collective-permute-start.40 = (f32[512,8,128]{2,0,1:T(8,128)S(1)}, f32[512,8,128]{2,0,1:T(8,128)S(1)}, u32[]{:S(2)}, u32[]{:S(2)}) collective-permute-start(f32[512,8,128]{2,0,1:T(8,128)S(1)} %bitcast_add_fusion.20), channel_id=1, source_target_pairs={{0,1},{1,2},{2,3},{3,4},{4,5},{5,6},{6,7},{7,8},{8,9},{9,10},{10,1... | collective-permute-start | bytes 6291464 | tf_op jit(solution)/shard_map/ppermute | solution.py:63
  743.3 126.9 %collective-permute-start.26 = (bf16[512,8,128]{2,0,1:T(8,128)(2,1)S(1)}, bf16[512,8,128]{2,0,1:T(8,128)(2,1)S(1)}, u32[]{:S(2)}, u32[]{:S(2)}) collective-permute-start(bf16[512,8,128]{2,0,1:T(8,128)(2,1)S(1)} %collective-permute-done.24), channel_id=1, source_target_pairs={{0,1},{1,2},{2,3},{3,4},{4,5},{5,6},{6,7},{7,8},{8,9},{9,10},{10,1... | collective-permute-start | bytes 3145736 | tf_op jit(solution)/shard_map/ppermute | solution.py:61
  754.0 116.2 %collective-permute-start.27 = (bf16[512,8,128]{2,0,1:T(8,128)(2,1)}, bf16[512,8,128]{2,0,1:T(8,128)(2,1)}, u32[]{:S(2)}, u32[]{:S(2)}) collective-permute-start(bf16[512,8,128]{2,0,1:T(8,128)(2,1)} %collective-permute-done.25), channel_id=1, source_target_pairs={{0,1},{1,2},{2,3},{3,4},{4,5},{5,6},{6,7},{7,8},{8,9},{9,10},{10,1... | collective-permute-start | bytes 3145736 | tf_op jit(solution)/shard_map/ppermute | solution.py:62
  778.1 65.8 %collective-permute-start.41 = (f32[512,8,128]{2,0,1:T(8,128)}, f32[512,8,128]{2,0,1:T(8,128)}, u32[]{:S(2)}, u32[]{:S(2)}) collective-permute-start(f32[512,8,128]{2,0,1:T(8,128)} %bitcast_add_fusion.19), channel_id=1, source_target_pairs={{0,1},{1,2},{2,3},{3,4},{4,5},{5,6},{6,7},{7,8},{8,9},{9,10},{10,1... | collective-permute-start | bytes 6291464 | tf_op jit(solution)/shard_map/ppermute | solution.py:63
  870.2 110.3 %collective-permute-start.29 = (bf16[512,8,128]{2,0,1:T(8,128)(2,1)}, bf16[512,8,128]{2,0,1:T(8,128)(2,1)}, u32[]{:S(2)}, u32[]{:S(2)}) collective-permute-start(bf16[512,8,128]{2,0,1:T(8,128)(2,1)} %collective-permute-done.27), channel_id=1, source_target_pairs={{0,1},{1,2},{2,3},{3,4},{4,5},{5,6},{6,7},{7,8},{8,9},{9,10},{10,1... | collective-permute-start | bytes 3145736 | tf_op jit(solution)/shard_map/ppermute | solution.py:62
  890.7 65.5 %collective-permute-start.43 = (f32[512,8,128]{2,0,1:T(8,128)S(1)}, f32[512,8,128]{2,0,1:T(8,128)S(1)}, u32[]{:S(2)}, u32[]{:S(2)}) collective-permute-start(f32[512,8,128]{2,0,1:T(8,128)S(1)} %bitcast_add_fusion.17), channel_id=1, source_target_pairs={{0,1},{1,2},{2,3},{3,4},{4,5},{5,6},{6,7},{7,8},{8,9},{9,10},{10,1... | collective-permute-start | bytes 6291464 | tf_op jit(solution)/shard_map/ppermute | solution.py:63
  913.3 65.5 %collective-permute-start.59 = (f32[512,8,128]{2,0,1:T(8,128)S(1)}, f32[512,8,128]{2,0,1:T(8,128)S(1)}, u32[]{:S(2)}, u32[]{:S(2)}) collective-permute-start(f32[512,8,128]{2,0,1:T(8,128)S(1)} %bitcast_add_fusion.2), channel_id=1, source_target_pairs={{0,1},{1,2},{2,3},{3,4},{4,5},{5,6},{6,7},{7,8},{8,9},{9,10},{10,1... | collective-permute-start | bytes 6291464 | tf_op jit(solution)/shard_map/ppermute | solution.py:64
  (82 other events, 2629.8 us)
where the time goes:
time: 1060 us; the launch traced here: 1050 us
  waiting for transfers between devices  687 us (65%)
  matrix products  263 us (25%)
  other arithmetic  71.8 us (7%)
  local copies, waits for them, and re-layouts  13.8 us (1%)
  starting transfers between devices  11.7 us (1%)
    ppermute x16, waiting for transfers between devices, local(): gv = lax.ppermute(gv, 'cp', perm)  214 us
    ppermute x16, waiting for transfers between devices, local(): gk = lax.ppermute(gk, 'cp', perm)  212 us
    ppermute x15, waiting for transfers between devices, local(): kb = lax.ppermute(kb, 'cp', perm)  177 us
    ppermute x15, waiting for transfers between devices, local(): vb = lax.ppermute(vb, 'cp', perm)  84.8 us
    dot_general x16, matrix products, body(): dp = jnp.einsum('qhd,khd->hqk', dt, vb, preferred_element_type=f32)  77.8 us
    dot_general x16, matrix products, body(): jnp.einsum('hqk,qhd->khd', p.astype(jnp.bfloat16), dt, preferred_element_...  77.8 us
    dot_general x16, matrix products, body(): dq = jnp.einsum('hqk,khd->qhd', ds, kb, preferred_element_type=f32) * scale  51.3 us
    add x14, other arithmetic, body(): gv + jnp.einsum('hqk,qhd->khd', p.astype(jnp.bfloat16), dt, preferred_ele...  39.5 us
  transfers between devices with their start and end apart: 62, of which 40 were waited for; matrix products, arithmetic and copies ran while one was open for 33% of the time, Pallas kernels for 0%

commit v1 on v0

v1 whole, which is shorter than its diff:
```python
import functools
import math

import jax
import jax.numpy as jnp
from jax import lax
from jax.experimental import pallas as pl
from jax.experimental.pallas import tpu as pltpu
from jax.sharding import PartitionSpec as P

MESH = pl.DeviceIdType.MESH
F32 = jnp.float32
BF16 = jnp.bfloat16

CH = 8
R = 32
C = 16
KB = CH * R
QB = 2 * KB
D = 128
NT = (((1,), (1,)), ((), ()))
TN = (((0,), (0,)), ((), ()))
LOG2E = math.log2(math.e)
SCALE = D ** -0.5


def _kernel(q_ref, k_ref, v_ref, do_ref, stat_ref, dq_out, dk_out, dv_out,
            stage, buf, statbuf, rows, dq, dqin, dqs, kvs, rkv, rq, tmp, dk_acc, dv_acc,
            s_in, r_in, s_fw, r_fw, s_kv, r_kv, s_x, r_x, s_q, r_q, s_st, r_st):
    cp = lax.axis_index('cp')
    chip = cp // 2
    core = cp % 2
    sib = {'cp': chip * 2 + 1 - core}

    def peer(i):
        return lax.rem(chip + i, CH)

    def dev(h):
        return {'cp': h * 2 + core}

    def rcopy(src, dst, ss, rs, to):
        return pltpu.make_async_remote_copy(src_ref=src, dst_ref=dst, send_sem=ss, recv_sem=rs,
                                            device_id=to, device_id_type=MESH)

    barrier = pltpu.get_barrier_semaphore()
    pl.semaphore_signal(barrier, inc=1, device_id=sib, device_id_type=MESH)
    for i in range(1, CH):
        pl.semaphore_signal(barrier, inc=1, device_id=dev(peer(i)), device_id_type=MESH)
    pl.semaphore_wait(barrier, CH)

    statbuf[core, chip] = stat_ref[chip]
    for i in range(1, CH):
        h = peer(i)
        rcopy(stat_ref.at[h], statbuf.at[core, chip], s_st.at[0], r_st.at[0], dev(h)).start()

    def gather(c):
        for t, ref in enumerate((k_ref, v_ref, q_ref, do_ref)):
            tmp[t] = ref[pl.ds(pl.multiple_of(c * KB, KB), KB), :].astype(F32)
            for h in range(CH):
                stage[c, h, t] = tmp[t, pl.ds(h, R, stride=CH), :].astype(BF16)
        buf[c, core, chip] = stage[c, chip]

    def send(c):
        for i in range(1, CH):
            h = peer(i)
            rcopy(stage.at[c, h], buf.at[c, core, chip], s_in.at[c], r_in.at[c], dev(h)).start()

    gather(C - 1)

    def prologue(n, _):
        c = C - 1 - n

        @pl.when(c > 0)
        def _():
            gather(c - 1)
        send(c)
        return 0

    lax.fori_loop(0, C, prologue, 0)

    rcopy(statbuf.at[core, pl.ds(0, CH - 1)], statbuf.at[core, pl.ds(0, CH - 1)],
          s_st.at[0], r_st.at[0], sib).wait_recv()
    fst = rcopy(statbuf.at[core], statbuf.at[core], s_st.at[1], r_st.at[1], sib)
    fst.start()
    rcopy(statbuf.at[1 - core], statbuf.at[1 - core], s_st.at[1], r_st.at[1], sib).wait_recv()
    quarter = lax.broadcasted_iota(jnp.int32, (1, 128), 1) // R
    for st in range(2):
        mul = LOG2E if st == 0 else 1.0
        for t in range(4):
            for g in range(4):
                src = [statbuf[g // 2, (g % 2) * 4 + m, :, st * 512 + t * 128:st * 512 + t * 128 + 128] * mul
                       for m in range(4)]
                for r in range(4):
                    acc = jnp.zeros((1, 128), F32)
                    for m in range(4):
                        sh = ((m - r) % 4) * R
                        x = pltpu.roll(src[m], sh, 1) if sh else src[m]
                        acc = jnp.where(quarter == m, x, acc)
                    rows[4 * t + r, st:st + 1, g * 128:(g + 1) * 128] = acc

    def diag_mask():
        ki = lax.broadcasted_iota(jnp.int32, (KB, QB), 0)
        qi = lax.broadcasted_iota(jnp.int32, (KB, QB), 1)
        kpos = (ki % R) * 16 + (ki // R) * 2 + core
        qpos = (qi % R) * 16 + ((qi // R) % CH) * 2 + qi // KB
        return kpos <= qpos

    def tile(c, b, diag):
        kk = buf[c, core, :, 0].reshape(KB, D)
        vv = buf[c, core, :, 1].reshape(KB, D)
        qq = buf[b, :, :, 2].reshape(QB, D)
        dd = buf[b, :, :, 3].reshape(QB, D)
        s = lax.dot_general(kk, qq, NT, preferred_element_type=F32)
        p = jnp.exp2(s * (SCALE * LOG2E) - rows[b, 0:1, :])
        if diag:
            p = jnp.where(diag_mask(), p, 0.0)
        dp = lax.dot_general(vv, dd, NT, preferred_element_type=F32)
        dv = jnp.dot(p.astype(BF16), dd, preferred_element_type=F32)
        ds = (p * (dp - rows[b, 1:2, :])).astype(BF16)
        dk = jnp.dot(ds, qq, preferred_element_type=F32)
        dqb = lax.dot_general(ds, kk, TN, preferred_element_type=F32)
        if diag:
            dv_acc[...] = dv
            dk_acc[...] = dk
            dq[b] = dqb.reshape(2, KB, D)
        else:
            dv_acc[...] += dv
            dk_acc[...] += dk
            dq[b] += dqb.reshape(2, KB, D)

    def arrive(c):
        rcopy(buf.at[c, core, pl.ds(0, CH - 1)], buf.at[c, core, pl.ds(0, CH - 1)],
              s_in.at[c], r_in.at[c], sib).wait_recv()
        rcopy(buf.at[c, core, :, pl.ds(2, 2)], buf.at[c, core, :, pl.ds(2, 2)],
              s_fw.at[c], r_fw.at[c], sib).start()

    def forwarded(c):
        return rcopy(buf.at[c, 1 - core, :, pl.ds(2, 2)], buf.at[c, 1 - core, :, pl.ds(2, 2)],
                     s_fw.at[c], r_fw.at[c], sib)

    def give_kv(c):
        kvs[c, :, 0] = (dk_acc[...] * SCALE).astype(BF16).reshape(CH, R, D)
        kvs[c, :, 1] = dv_acc[...].astype(BF16).reshape(CH, R, D)
        rkv[c, chip] = kvs[c, chip]
        for i in range(1, CH):
            h = peer(i)
            rcopy(kvs.at[c, h], rkv.at[c, chip], s_kv.at[c], r_kv.at[c], dev(h)).start()

    def step(n, _):
        c = C - 1 - n
        arrive(c)
        forwarded(c).wait_recv()
        tile(c, c, True)
        lax.fori_loop(c + 1, C, lambda b, _: (tile(c, b, False), 0)[1], 0)
        give_kv(c)
        return 0

    lax.fori_loop(0, C - 1, step, 0)

    def swap(b):
        rcopy(dq.at[b, 1 - core], dqin.at[b], s_x.at[b], r_x.at[b], sib).start()

    def give_q(b):
        rcopy(dq.at[b, core], dqin.at[b], s_x.at[b], r_x.at[b], sib).wait_recv()
        dqs[b] = ((dq[b, core] + dqin[b]) * SCALE).astype(BF16).reshape(CH, R, D)
        rq[b, chip] = dqs[b, chip]
        for i in range(1, CH):
            h = peer(i)
            rcopy(dqs.at[b, h], rq.at[b, chip], s_q.at[b], r_q.at[b], dev(h)).start()

    arrive(0)
    forwarded(0).wait_recv()
    tile(0, 0, True)
    swap(0)

    def last(b, _):
        tile(0, b, False)
        swap(b)
        give_q(b - 1)
        return 0

    lax.fori_loop(1, C, last, 0)
    give_kv(0)
    give_q(C - 1)

    def put_kv(n, _):
        c = C - 1 - n
        rcopy(kvs.at[c, pl.ds(0, CH - 1)], rkv.at[c, pl.ds(0, CH - 1)], s_kv.at[c], r_kv.at[c], sib).wait_recv()
        for t, ref in enumerate((dk_out, dv_out)):
            for h in range(CH):
                tmp[t, pl.ds(h, R, stride=CH), :] = rkv[c, h, t].astype(F32)
            ref[pl.ds(pl.multiple_of(c * KB, KB), KB), :] = tmp[t].astype(BF16)
        return 0

    lax.fori_loop(0, C, put_kv, 0)

    def put_q(c, _):
        rcopy(dqs.at[c, pl.ds(0, CH - 1)], rq.at[c, pl.ds(0, CH - 1)], s_q.at[c], r_q.at[c], sib).wait_recv()
        for h in range(CH):
            tmp[2, pl.ds(h, R, stride=CH), :] = rq[c, h].astype(F32)
        dq_out[pl.ds(pl.multiple_of(c * KB, KB), KB), :] = tmp[2].astype(BF16)
        return 0

    lax.fori_loop(0, C, put_q, 0)

    rcopy(statbuf.at[core, pl.ds(0, CH - 1)], statbuf.at[core, pl.ds(0, CH - 1)],
          s_st.at[0], r_st.at[0], sib).wait_send()
    fst.wait_send()

    def drain(c, _):
        rcopy(stage.at[c, pl.ds(0, CH - 1)], buf.at[c, core, pl.ds(0, CH - 1)], s_in.at[c], r_in.at[c], sib).wait_send()
        forwarded(c).wait_send()
        rcopy(kvs.at[c, pl.ds(0, CH - 1)], rkv.at[c, pl.ds(0, CH - 1)], s_kv.at[c], r_kv.at[c], sib).wait_send()
        rcopy(dq.at[c, core], dqin.at[c], s_x.at[c], r_x.at[c], sib).wait_send()
        rcopy(dqs.at[c, pl.ds(0, CH - 1)], rq.at[c, pl.ds(0, CH - 1)], s_q.at[c], r_q.at[c], sib).wait_send()
        return 0

    lax.fori_loop(0, C, drain, 0)


def solution(mesh):
    rows = P(('data', 'cp'))
    cols = P(None, ('data', 'cp'))

    def local(q, k, v, o, dout, lse):
        c, h, d = q.shape
        dd = jnp.einsum('qhd,qhd->hq', dout, o, preferred_element_type=F32)
        stat = jnp.concatenate([lse, dd], axis=1).reshape(h, 1, 2 * c)
        flat = lambda x: x.reshape(c * h, d)
        vm = pl.BlockSpec(memory_space=pltpu.VMEM)
        sem = pltpu.SemaphoreType.DMA
        outs = pl.pallas_call(
            _kernel,
            out_shape=[jax.ShapeDtypeStruct((c * h, d), BF16)] * 3,
            in_specs=[vm] * 5,
            out_specs=[vm] * 3,
            scratch_shapes=[
                pltpu.VMEM((C, CH, 4, R, D), BF16),
                pltpu.VMEM((C, 2, CH, 4, R, D), BF16),
                pltpu.VMEM((2, CH, 1, 2 * c), F32),
                pltpu.VMEM((C, 8, QB), F32),
                pltpu.VMEM((C, 2, KB, D), F32),
                pltpu.VMEM((C, KB, D), F32),
                pltpu.VMEM((C, CH, R, D), BF16),
                pltpu.VMEM((C, CH, 2, R, D), BF16),
                pltpu.VMEM((C, CH, 2, R, D), BF16),
                pltpu.VMEM((C, CH, R, D), BF16),
                pltpu.VMEM((4, KB, D), F32),
                pltpu.VMEM((KB, D), F32),
                pltpu.VMEM((KB, D), F32),
            ] + [sem((C,))] * 10 + [sem((2,))] * 2,
            compiler_params=pltpu.CompilerParams(collective_id=0, has_side_effects=True,
                                                 vmem_limit_bytes=60 * 2 ** 20),
        )(flat(q), flat(k), flat(v), flat(dout), stat)
        return tuple(x.reshape(c, h, d) for x in outs)

    return jax.shard_map(local, mesh=mesh, in_specs=(rows, rows, rows, rows, rows, cols),
                         out_specs=(rows, rows, rows), check_vma=False)
```

time: 1060 us -> 194 us (0.18)
  waiting for transfers between devices: 687 us -> 0 us
  matrix products: 263 us -> 0 us
  Pallas kernels: 0 us -> 185 us
  other arithmetic: 71.8 us -> 2.17 us
  starting transfers between devices: 11.7 us -> 0 us
    ppermute x62 -> x0, waiting for transfers between devices: 687 us -> none  [the longest x16 214 us: local(): gv = lax.ppermute(gv, 'cp', perm)]
    dot_general x80 -> x0, matrix products: 263 us -> none  [the longest x16 77.8 us: body(): dp = jnp.einsum('qhd,khd->hqk', dt, vb, preferred_element_type=f32)]
    pallas_call x0 -> x1, Pallas kernels: none -> 185 us  [local(): pl.pallas_call(_kernel, out_shape=[jax.ShapeDtypeStruct((c * h, d), BF16)...]
    add x37 -> x0, other arithmetic: 66.2 us -> none  [the longest x14 39.5 us: body(): gv + jnp.einsum('hqk,qhd->khd', p.astype(jnp.bfloat16), dt, preferred_ele...]
    ppermute x62 -> x0, starting transfers between devices: 11.7 us -> none  [the longest x15 5.06 us: local(): vb = lax.ppermute(vb, 'cp', perm)]
  transfers between devices with their start and end apart: 62 -> 0, of which waited for: 40 -> 0; matrix products, arithmetic and copies ran while one was open for 33% -> 0% of each run, Pallas kernels for 0% -> 0%
where the time goes in v1:
time: 194 us
  Pallas kernels  185 us (95%)
  local copies, waits for them, and re-layouts  5.67 us (3%)
  other arithmetic  2.17 us (1%)
    pallas_call x1, Pallas kernels, local(): pl.pallas_call(_kernel, out_shape=[jax.ShapeDtypeStruct((c * h, d), BF16)...  185 us
    unnamed x9, local copies, waits for them, and re-layouts  4.93 us

profile of v1, /device:TPU:0, one launch (start us, length us, event | category | flops | bytes accessed | tf_op | source)
XLA Modules:
  0.0 193.8 jit_solution(6651411139245658881)
XLA Ops:
  0.6 0.0 copy-start.2
  0.6 2.2 %fusion = f32[8,512]{0,1:T(8,128)S(1)} fusion(bf16[512,8,128]{2,1,0:T(8,128)(2,1)} %param.9, bf16[512,8,128]{2,1,0:T(8,128)(2,1)} %param.10), kind=kLoop, calls=%fused_computation.1 | loop fusion | flops 2093056 | bytes 2113536
  2.8 0.1 copy.15
  2.9 0.0 copy-done.2
  2.9 0.7 reshape.34.stat_ref
  3.6 185.3 %shard_map.85 = (bf16[4096,128]{1,0:T(8,128)(2,1)}, bf16[4096,128]{1,0:T(8,128)(2,1)}, bf16[4096,128]{1,0:T(8,128)(2,1)}) custom-call(bf16[4096,128]{1,0:T(8,128)(2,1)} %bitcast.15, bf16[4096,128]{1,0:T(8,128)(2,1)} %bitcast.16, bf16[4096,128]{1,0:T(8,128)(2,1)} %bitcast.17, bf16[4096,128]{1,0:T(8,128)(2,1)} %bitcast.11, f32[8,1,1024]{2,1,0:T(1,128)} %reshape.34.stat_ref), custom_call_target="tpu_custom_call" | custom-call | tf_op jit(solution)/shard_map/pallas_call | solution.py:232
  188.8 0.0 copy-start.1
  188.9 2.4 %copy.20 = bf16[512,8,128]{2,1,0:T(8,128)(2,1)} copy(bf16[512,8,128]{2,1,0:T(8,128)(2,1)} %bitcast.14) | data formatting | bytes 2097152
  191.2 0.0 copy-done.1
  191.2 0.0 copy-start
  191.2 1.0 copy.21
  192.2 0.6 copy-done
  192.8 1.0 copy.22
  (1 shorter events, 0.0 us)
Async XLA Ops:
  0.6 2.3 %copy-start.2 = (f32[8,512]{1,0:T(8,128)S(1)}, f32[8,512]{1,0:T(8,128)}, u32[]{:S(2)}) copy-start(f32[8,512]{1,0:T(8,128)} %param.11) | copy-start | bytes 49156
  188.8 2.4 %copy-start.1 = (bf16[4096,128]{1,0:T(8,128)(2,1)S(1)}, bf16[4096,128]{1,0:T(8,128)(2,1)}, u32[]{:S(2)}) copy-start(bf16[4096,128]{1,0:T(8,128)(2,1)} %get-tuple-element.7) | copy-start | bytes 3145732
  191.2 1.6 copy-start

commit v2 on v1

v2 whole, which is shorter than its diff:
```python
import functools
import math

import jax
import jax.numpy as jnp
from jax import lax
from jax.experimental import pallas as pl
from jax.experimental.pallas import tpu as pltpu
from jax.sharding import PartitionSpec as P

MESH = pl.DeviceIdType.MESH
F32 = jnp.float32
BF16 = jnp.bfloat16

CH = 8
R = 32
C = 16
KB = CH * R
QB = 2 * KB
D = 128
NT = (((1,), (1,)), ((), ()))
TN = (((0,), (0,)), ((), ()))
LOG2E = math.log2(math.e)
U = 4
SCALE = D ** -0.5


def _kernel(k_hbm, v_hbm, q_hbm, do_hbm, o_hbm, lse_hbm, dq_out, dk_out, dv_out,
            xin, lsev, stage, ostage, statloc, buf, statbuf, rows, dq, dqin, dqs, kvs, rkv, rq, tmp, dk_acc, dv_acc,
            s_in, r_in, s_fw, r_fw, s_kv, r_kv, s_x, r_x, s_q, r_q, s_st, r_st, s_ld):
    cp = lax.axis_index('cp')
    chip = cp // 2
    core = cp % 2
    sib = {'cp': chip * 2 + 1 - core}

    hbm = (k_hbm, v_hbm, q_hbm, do_hbm, o_hbm)
    lead = (C - 1) * KB
    loads = []
    for t in range(4):
        loads.append(pltpu.make_async_copy(hbm[t].at[pl.ds(lead, KB)], xin.at[t, pl.ds(lead, KB)], s_ld.at[0, t]))
    for t in range(4):
        loads.append(pltpu.make_async_copy(hbm[t].at[pl.ds(0, lead)], xin.at[t, pl.ds(0, lead)], s_ld.at[1, t]))
    loads.append(pltpu.make_async_copy(o_hbm, xin.at[4], s_ld.at[0, 4]))
    loads.append(pltpu.make_async_copy(lse_hbm, lsev, s_ld.at[1, 4]))
    for x in loads:
        x.start()

    def peer(i):
        return lax.rem(chip + i, CH)

    def dev(h):
        return {'cp': h * 2 + core}

    def rcopy(src, dst, ss, rs, to):
        return pltpu.make_async_remote_copy(src_ref=src, dst_ref=dst, send_sem=ss, recv_sem=rs,
                                            device_id=to, device_id_type=MESH)

    def gather(c):
        r0 = pl.multiple_of(c * KB, KB)
        for t in range(4):
            tmp[t] = xin[t, pl.ds(r0, KB), :].astype(F32)
            for h in range(CH):
                stage[c, h, t] = tmp[t, pl.ds(h, R, stride=CH), :].astype(BF16)
        buf[c, core, chip] = stage[c, chip]

    def gather_o(c):
        tmp[4] = xin[4, pl.ds(pl.multiple_of(c * KB, KB), KB), :].astype(F32)
        for h in range(CH):
            ostage[c, h] = tmp[4, pl.ds(h, R, stride=CH), :].astype(BF16)

    def send(c):
        for i in range(1, CH):
            h = peer(i)
            rcopy(stage.at[c, h], buf.at[c, core, chip], s_in.at[c], r_in.at[c], dev(h)).start()

    def loop(lo, hi, f):
        lax.fori_loop(lo, hi, lambda x, _: (f(x), 0)[1], 0)

    barrier = pltpu.get_barrier_semaphore()
    pl.semaphore_signal(barrier, inc=1, device_id=sib, device_id_type=MESH)
    for i in range(1, CH):
        pl.semaphore_signal(barrier, inc=1, device_id=dev(peer(i)), device_id_type=MESH)
    for x in loads[:4]:
        x.wait()
    gather(C - 1)
    pl.semaphore_wait(barrier, CH)
    send(C - 1)
    for x in loads[4:]:
        x.wait()
    gather(C - 2)
    gather(C - 3)
    send(C - 2)
    gather(C - 4)
    send(C - 3)
    loop(0, C - 4, lambda n: gather(C - 5 - n))
    send(C - 4)
    loop(0, C, gather_o)

    ones = jnp.ones((8, D), BF16)
    for h in range(CH):
        x = (stage[:, h, 3].astype(F32) * ostage[:, h].astype(F32)).reshape(C * R, D)
        hi = x.astype(BF16)
        lo = (x - hi.astype(F32)).astype(BF16)
        e = (lax.dot_general(ones, hi, NT, preferred_element_type=F32)
             + lax.dot_general(ones, lo, NT, preferred_element_type=F32))
        statloc[h, :, :C * R] = lsev[h:h + 1, :]
        statloc[h, :, C * R:] = e[0:1, :]
    statbuf[core, chip] = statloc[chip]
    for i in range(1, CH):
        h = peer(i)
        rcopy(statloc.at[h], statbuf.at[core, chip], s_st.at[0], r_st.at[0], dev(h)).start()
    loop(0, C - 4, lambda n: send(C - 5 - n))

    def arrive(c):
        rcopy(buf.at[c, core, pl.ds(0, CH - 1)], buf.at[c, core, pl.ds(0, CH - 1)],
              s_in.at[c], r_in.at[c], sib).wait_recv()
        rcopy(buf.at[c, core, :, pl.ds(2, 2)], buf.at[c, core, :, pl.ds(2, 2)],
              s_fw.at[c], r_fw.at[c], sib).start()

    def forwarded(c):
        return rcopy(buf.at[c, 1 - core, :, pl.ds(2, 2)], buf.at[c, 1 - core, :, pl.ds(2, 2)],
                     s_fw.at[c], r_fw.at[c], sib)

    arrive(C - 1)
    rcopy(statbuf.at[core, pl.ds(0, CH - 1)], statbuf.at[core, pl.ds(0, CH - 1)],
          s_st.at[0], r_st.at[0], sib).wait_recv()
    fst = rcopy(statbuf.at[core], statbuf.at[core], s_st.at[1], r_st.at[1], sib)
    fst.start()
    rcopy(statbuf.at[1 - core], statbuf.at[1 - core], s_st.at[1], r_st.at[1], sib).wait_recv()
    quarter = lax.broadcasted_iota(jnp.int32, (1, 128), 1) // R
    for st in range(2):
        mul = LOG2E if st == 0 else 1.0
        for t in range(4):
            for g in range(4):
                src = [statbuf[g // 2, (g % 2) * 4 + m, :, st * 512 + t * 128:st * 512 + t * 128 + 128] * mul
                       for m in range(4)]
                for r in range(4):
                    acc = jnp.zeros((1, 128), F32)
                    for m in range(4):
                        sh = ((m - r) % 4) * R
                        x = pltpu.roll(src[m], sh, 1) if sh else src[m]
                        acc = jnp.where(quarter == m, x, acc)
                    rows[4 * t + r, st:st + 1, g * 128:(g + 1) * 128] = acc

    def diag_mask():
        ki = lax.broadcasted_iota(jnp.int32, (KB, QB), 0)
        qi = lax.broadcasted_iota(jnp.int32, (KB, QB), 1)
        kpos = (ki % R) * 16 + (ki // R) * 2 + core
        qpos = (qi % R) * 16 + ((qi // R) % CH) * 2 + qi // KB
        return kpos <= qpos

    def clear():
        dk_acc[...] = jnp.zeros_like(dk_acc)
        dv_acc[...] = jnp.zeros_like(dv_acc)

    def tile(c, b, diag):
        kk = buf[c, core, :, 0].reshape(KB, D)
        vv = buf[c, core, :, 1].reshape(KB, D)
        qq = buf[b, :, :, 2].reshape(QB, D)
        dd = buf[b, :, :, 3].reshape(QB, D)
        s = lax.dot_general(kk, qq, NT, preferred_element_type=F32)
        p = jnp.exp2(s * (SCALE * LOG2E) - rows[b, 0:1, :])
        if diag:
            p = jnp.where(diag_mask(), p, 0.0)
        dp = lax.dot_general(vv, dd, NT, preferred_element_type=F32)
        dv_acc[...] += jnp.dot(p.astype(BF16), dd, preferred_element_type=F32)
        ds = (p * (dp - rows[b, 1:2, :])).astype(BF16)
        dk_acc[...] += jnp.dot(ds, qq, preferred_element_type=F32)
        dqt = lax.dot_general(kk, ds, TN, preferred_element_type=F32)
        for y in range(2):
            part = dqt[:, y * KB:(y + 1) * KB]
            if diag:
                dq[b, y] = part
            else:
                dq[b, y] += part

    def send_kv(c):
        for i in range(1, CH):
            h = peer(i)
            rcopy(kvs.at[c, h], rkv.at[c, chip], s_kv.at[c], r_kv.at[c], dev(h)).start()

    def make_kv(c):
        kvs[c, :, 0] = (dk_acc[...] * SCALE).astype(BF16).reshape(CH, R, D)
        kvs[c, :, 1] = dv_acc[...].astype(BF16).reshape(CH, R, D)
        rkv[c, chip] = kvs[c, chip]

    def step(n):
        c = C - 1 - n
        forwarded(c).wait_recv()
        clear()
        whole = n // U
        loop(0, whole, lambda u: [tile(c, c + 1 + U * u + x, False) for x in range(U)])
        loop(c + 1 + whole * U, C, lambda b: tile(c, b, False))
        arrive(c - 1)
        tile(c, c, True)
        make_kv(c)
        send_kv(c)

    loop(0, C - 1, step)

    def swap(b):
        rcopy(dq.at[b, 1 - core], dqin.at[b], s_x.at[b], r_x.at[b], sib).start()

    def give_q(b):
        rcopy(dq.at[b, core], dqin.at[b], s_x.at[b], r_x.at[b], sib).wait_recv()
        dqs[b] = ((dq[b, core] + dqin[b]) * SCALE).T.astype(BF16).reshape(CH, R, D)
        rq[b, chip] = dqs[b, chip]
        for i in range(1, CH):
            h = peer(i)
            rcopy(dqs.at[b, h], rq.at[b, chip], s_q.at[b], r_q.at[b], dev(h)).start()

    forwarded(0).wait_recv()
    clear()
    tile(0, 0, True)
    tile(0, 1, False)
    swap(0)
    swap(1)

    def last(u):
        tile(0, 2 * u, False)
        tile(0, 2 * u + 1, False)
        swap(2 * u)
        swap(2 * u + 1)

        @pl.when(u >= 2)
        def _():
            give_q(2 * u - 4)
            give_q(2 * u - 3)

    loop(1, C // 2, last)
    make_kv(0)
    send_kv(0)
    loop(C - 4, C, give_q)

    def put_kv(n):
        c = C - 1 - n
        rcopy(kvs.at[c, pl.ds(0, CH - 1)], rkv.at[c, pl.ds(0, CH - 1)], s_kv.at[c], r_kv.at[c], sib).wait_recv()
        for t, ref in enumerate((dk_out, dv_out)):
            for h in range(CH):
                tmp[t, pl.ds(h, R, stride=CH), :] = rkv[c, h, t].astype(F32)
            ref[pl.ds(pl.multiple_of(c * KB, KB), KB), :] = tmp[t].astype(BF16)

    loop(0, C, put_kv)

    def put_q(c):
        rcopy(dqs.at[c, pl.ds(0, CH - 1)], rq.at[c, pl.ds(0, CH - 1)], s_q.at[c], r_q.at[c], sib).wait_recv()
        for h in range(CH):
            tmp[2, pl.ds(h, R, stride=CH), :] = rq[c, h].astype(F32)
        dq_out[pl.ds(pl.multiple_of(c * KB, KB), KB), :] = tmp[2].astype(BF16)

    def drain(c):
        rcopy(stage.at[c, pl.ds(0, CH - 1)], buf.at[c, core, pl.ds(0, CH - 1)], s_in.at[c], r_in.at[c], sib).wait_send()
        forwarded(c).wait_send()
        rcopy(kvs.at[c, pl.ds(0, CH - 1)], rkv.at[c, pl.ds(0, CH - 1)], s_kv.at[c], r_kv.at[c], sib).wait_send()
        rcopy(dq.at[c, core], dqin.at[c], s_x.at[c], r_x.at[c], sib).wait_send()

    def drain_q(c):
        rcopy(dqs.at[c, pl.ds(0, CH - 1)], rq.at[c, pl.ds(0, CH - 1)], s_q.at[c], r_q.at[c], sib).wait_send()

    rcopy(statbuf.at[core, pl.ds(0, CH - 1)], statbuf.at[core, pl.ds(0, CH - 1)],
          s_st.at[0], r_st.at[0], sib).wait_send()
    fst.wait_send()
    loop(0, C, put_q)
    loop(0, C, drain)
    loop(0, C, drain_q)


def _write(dq_ref, dk_ref, dv_ref, dq_hbm, dk_hbm, dv_hbm, sem):
    copies = [pltpu.make_async_copy(a, b, sem.at[i])
              for i, (a, b) in enumerate(((dq_ref, dq_hbm), (dk_ref, dk_hbm), (dv_ref, dv_hbm)))]
    for x in copies:
        x.start()
    for x in copies:
        x.wait()


def solution(mesh):
    rows = P(('data', 'cp'))
    cols = P(None, ('data', 'cp'))

    def local(q, k, v, o, dout, lse):
        c, h, d = q.shape
        flat = lambda x: x.reshape(c * h, d)
        vm = pl.BlockSpec(memory_space=pltpu.VMEM)
        hbm = pl.BlockSpec(memory_space=pltpu.HBM)
        sem = pltpu.SemaphoreType.DMA
        outs = pl.pallas_call(
            _kernel,
            out_shape=[pltpu.VMEM((c * h, d), BF16)] * 3,
            in_specs=[hbm] * 6,
            out_specs=[vm] * 3,
            scratch_shapes=[
                pltpu.VMEM((5, c * h, d), BF16),
                pltpu.VMEM((h, c), F32),
                pltpu.VMEM((C, CH, 4, R, D), BF16),
                pltpu.VMEM((C, CH, R, D), BF16),
                pltpu.VMEM((CH, 1, 2 * c), F32),
                pltpu.VMEM((C, 2, CH, 4, R, D), BF16),
                pltpu.VMEM((2, CH, 1, 2 * c), F32),
                pltpu.VMEM((C, 8, QB), F32),
                pltpu.VMEM((C, 2, D, KB), F32),
                pltpu.VMEM((C, D, KB), F32),
                pltpu.VMEM((C, CH, R, D), BF16),
                pltpu.VMEM((C, CH, 2, R, D), BF16),
                pltpu.VMEM((C, CH, 2, R, D), BF16),
                pltpu.VMEM((C, CH, R, D), BF16),
                pltpu.VMEM((5, KB, D), F32),
                pltpu.VMEM((KB, D), F32),
                pltpu.VMEM((KB, D), F32),
            ] + [sem((C,))] * 10 + [sem((2,))] * 2 + [sem((2, 5))],
            compiler_params=pltpu.CompilerParams(collective_id=0, has_side_effects=True,
                                                 vmem_limit_bytes=40 * 2 ** 20),
        )(*[pltpu.with_memory_space_constraint(x, pltpu.HBM) for x in (flat(k), flat(v), flat(q), flat(dout), flat(o), lse)])
        outs = pl.pallas_call(
            _write,
            out_shape=[jax.ShapeDtypeStruct((c * h, d), BF16)] * 3,
            in_specs=[vm] * 3,
            out_specs=[hbm] * 3,
            scratch_shapes=[sem((3,))],
            compiler_params=pltpu.CompilerParams(vmem_limit_bytes=2 ** 20),
        )(*[pltpu.with_memory_space_constraint(x, pltpu.VMEM) for x in outs])
        return tuple(x.reshape(c, h, d) for x in outs)

    return jax.shard_map(local, mesh=mesh, in_specs=(rows, rows, rows, rows, rows, cols),
                         out_specs=(rows, rows, rows), check_vma=False)
```

time: 194 us -> 170 us (0.88)
  Pallas kernels: 185 us -> 169 us
  local copies, waits for them, and re-layouts: 5.67 us -> 0 us
  other arithmetic: 2.17 us -> 0 us
    pallas_call x1 -> x2, Pallas kernels: 185 us -> 169 us  [the longest x1 168 us: local(): pl.pallas_call(_kernel, out_shape=[pltpu.VMEM((c * h, d), BF16)] * 3, in_...]
    unnamed x9 -> x0, local copies, waits for them, and re-layouts: 4.93 us -> none
    unnamed x1 -> x0, other arithmetic: 2.17 us -> none
where the time goes in v2:
time: 170 us
  Pallas kernels  169 us (99%)
    pallas_call x1, Pallas kernels, local(): pl.pallas_call(_kernel, out_shape=[pltpu.VMEM((c * h, d), BF16)] * 3, in_...  168 us

profile of v2, /device:TPU:0, one launch (start us, length us, event | category | flops | bytes accessed | tf_op | source)
XLA Modules:
  0.0 170.1 jit_solution(3859496368448889050)
XLA Ops:
  0.6 167.7 %shard_map.85 = (bf16[4096,128]{1,0:T(8,128)(2,1)S(1)}, bf16[4096,128]{1,0:T(8,128)(2,1)S(1)}, bf16[4096,128]{1,0:T(8,128)(2,1)S(1)}) custom-call(bf16[4096,128]{1,0:T(8,128)(2,1)} %bitcast.8, bf16[4096,128]{1,0:T(8,128)(2,1)} %bitcast.9, bf16[4096,128]{1,0:T(8,128)(2,1)} %bitcast.10, bf16[4096,128]{1,0:T(8,128)(2,1)} %bitcast.11, ...), custom_call_target="tpu_custom_call" | custom-call | tf_op jit(solution)/shard_map/pallas_call | solution.py:287
  168.4 1.7 shard_map.86

commit v3 on v2

--- a/solution.py
+++ b/solution.py
@@ -22,6 +22,8 @@
 TN = (((0,), (0,)), ((), ()))
 LOG2E = math.log2(math.e)
 U = 4
+GK = 2
+GQ = 4
 SCALE = D ** -0.5
 
 
@@ -174,15 +176,17 @@
             else:
                 dq[b, y] += part
 
-    def send_kv(c):
+    def send_kv(g):
         for i in range(1, CH):
             h = peer(i)
-            rcopy(kvs.at[c, h], rkv.at[c, chip], s_kv.at[c], r_kv.at[c], dev(h)).start()
+            rcopy(kvs.at[g, h], rkv.at[g, chip], s_kv.at[g], r_kv.at[g], dev(h)).start()
 
     def make_kv(c):
-        kvs[c, :, 0] = (dk_acc[...] * SCALE).astype(BF16).reshape(CH, R, D)
-        kvs[c, :, 1] = dv_acc[...].astype(BF16).reshape(CH, R, D)
-        rkv[c, chip] = kvs[c, chip]
+        g = c // GK
+        x = c % GK
+        kvs[g, :, x, 0] = (dk_acc[...] * SCALE).astype(BF16).reshape(CH, R, D)
+        kvs[g, :, x, 1] = dv_acc[...].astype(BF16).reshape(CH, R, D)
+        rkv[g, chip, x] = kvs[g, chip, x]
 
     def step(n):
         c = C - 1 - n
@@ -194,7 +198,10 @@
         arrive(c - 1)
         tile(c, c, True)
         make_kv(c)
-        send_kv(c)
+
+        @pl.when(c % GK == 0)
+        def _():
+            send_kv(c // GK)
 
     loop(0, C - 1, step)
 
@@ -203,11 +210,15 @@
 
     def give_q(b):
         rcopy(dq.at[b, core], dqin.at[b], s_x.at[b], r_x.at[b], sib).wait_recv()
-        dqs[b] = ((dq[b, core] + dqin[b]) * SCALE).T.astype(BF16).reshape(CH, R, D)
-        rq[b, chip] = dqs[b, chip]
+        g = b // GQ
+        x = b % GQ
+        dqs[g, :, x] = ((dq[b, core] + dqin[b]) * SCALE).T.astype(BF16).reshape(CH, R, D)
+        rq[g, chip, x] = dqs[g, chip, x]
+
+    def send_q(g):
         for i in range(1, CH):
             h = peer(i)
-            rcopy(dqs.at[b, h], rq.at[b, chip], s_q.at[b], r_q.at[b], dev(h)).start()
+            rcopy(dqs.at[g, h], rq.at[g, chip], s_q.at[g], r_q.at[g], dev(h)).start()
 
     forwarded(0).wait_recv()
     clear()
@@ -227,42 +238,52 @@
             give_q(2 * u - 4)
             give_q(2 * u - 3)
 
+        @pl.when((u >= 2) & ((2 * u - 2) % GQ == 0))
+        def _():
+            send_q((2 * u - 2) // GQ - 1)
+
     loop(1, C // 2, last)
     make_kv(0)
     send_kv(0)
     loop(C - 4, C, give_q)
+    loop((C - 4) // GQ, C // GQ, send_q)
+
+    def all_kv(g):
+        return rcopy(kvs.at[g, pl.ds(0, CH - 1)], rkv.at[g, pl.ds(0, CH - 1)], s_kv.at[g], r_kv.at[g], sib)
+
+    def all_q(g):
+        return rcopy(dqs.at[g, pl.ds(0, CH - 1)], rq.at[g, pl.ds(0, CH - 1)], s_q.at[g], r_q.at[g], sib)
 
     def put_kv(n):
-        c = C - 1 - n
-        rcopy(kvs.at[c, pl.ds(0, CH - 1)], rkv.at[c, pl.ds(0, CH - 1)], s_kv.at[c], r_kv.at[c], sib).wait_recv()
-        for t, ref in enumerate((dk_out, dv_out)):
+        g = C // GK - 1 - n
+        all_kv(g).wait_recv()
+        for x in range(GK):
+            for t, ref in enumerate((dk_out, dv_out)):
+                for h in range(CH):
+                    tmp[t, pl.ds(h, R, stride=CH), :] = rkv[g, h, x, t].astype(F32)
+                ref[pl.ds(pl.multiple_of((g * GK + x) * KB, KB), KB), :] = tmp[t].astype(BF16)
+
+    loop(0, C // GK, put_kv)
+
+    def put_q(g):
+        all_q(g).wait_recv()
+        for x in range(GQ):
             for h in range(CH):
-                tmp[t, pl.ds(h, R, stride=CH), :] = rkv[c, h, t].astype(F32)
-            ref[pl.ds(pl.multiple_of(c * KB, KB), KB), :] = tmp[t].astype(BF16)
-
-    loop(0, C, put_kv)
-
-    def put_q(c):
-        rcopy(dqs.at[c, pl.ds(0, CH - 1)], rq.at[c, pl.ds(0, CH - 1)], s_q.at[c], r_q.at[c], sib).wait_recv()
-        for h in range(CH):
-            tmp[2, pl.ds(h, R, stride=CH), :] = rq[c, h].astype(F32)
-        dq_out[pl.ds(pl.multiple_of(c * KB, KB), KB), :] = tmp[2].astype(BF16)
+                tmp[x, pl.ds(h, R, stride=CH), :] = rq[g, h, x].astype(F32)
+            dq_out[pl.ds(pl.multiple_of((g * GQ + x) * KB, KB), KB), :] = tmp[x].astype(BF16)
 
     def drain(c):
         rcopy(stage.at[c, pl.ds(0, CH - 1)], buf.at[c, core, pl.ds(0, CH - 1)], s_in.at[c], r_in.at[c], sib).wait_send()
         forwarded(c).wait_send()
-        rcopy(kvs.at[c, pl.ds(0, CH - 1)], rkv.at[c, pl.ds(0, CH - 1)], s_kv.at[c], r_kv.at[c], sib).wait_send()
         rcopy(dq.at[c, core], dqin.at[c], s_x.at[c], r_x.at[c], sib).wait_send()
-
-    def drain_q(c):
-        rcopy(dqs.at[c, pl.ds(0, CH - 1)], rq.at[c, pl.ds(0, CH - 1)], s_q.at[c], r_q.at[c], sib).wait_send()
 
     rcopy(statbuf.at[core, pl.ds(0, CH - 1)], statbuf.at[core, pl.ds(0, CH - 1)],
           s_st.at[0], r_st.at[0], sib).wait_send()
     fst.wait_send()
-    loop(0, C, put_q)
     loop(0, C, drain)
-    loop(0, C, drain_q)
+    loop(0, C // GQ, put_q)
+    loop(0, C // GK, lambda g: all_kv(g).wait_send())
+    loop(0, C // GQ, lambda g: all_q(g).wait_send())
 
 
 def _write(dq_ref, dk_ref, dv_ref, dq_hbm, dk_hbm, dv_hbm, sem):
@@ -300,10 +321,10 @@
                 pltpu.VMEM((C, 8, QB), F32),
                 pltpu.VMEM((C, 2, D, KB), F32),
                 pltpu.VMEM((C, D, KB), F32),
-                pltpu.VMEM((C, CH, R, D), BF16),
-                pltpu.VMEM((C, CH, 2, R, D), BF16),
-                pltpu.VMEM((C, CH, 2, R, D), BF16),
-                pltpu.VMEM((C, CH, R, D), BF16),
+                pltpu.VMEM((C // GQ, CH, GQ, R, D), BF16),
+                pltpu.VMEM((C // GK, CH, GK, 2, R, D), BF16),
+                pltpu.VMEM((C // GK, CH, GK, 2, R, D), BF16),
+                pltpu.VMEM((C // GQ, CH, GQ, R, D), BF16),
                 pltpu.VMEM((5, KB, D), F32),
                 pltpu.VMEM((KB, D), F32),
                 pltpu.VMEM((KB, D), F32),

time: 170 us -> 168 us (0.988)
    pallas_call x1, Pallas kernels: 168 us -> 166 us  [local(): pl.pallas_call(_kernel, out_shape=[pltpu.VMEM((c * h, d), BF16)] * 3, in_...]
where the time goes in v3:
time: 168 us
  Pallas kernels  168 us (100%)
    pallas_call x1, Pallas kernels, local(): pl.pallas_call(_kernel, out_shape=[pltpu.VMEM((c * h, d), BF16)] * 3, in_...  166 us

profile of v3, /device:TPU:0, one launch (start us, length us, event | category | flops | bytes accessed | tf_op | source)
XLA Modules:
  0.0 168.2 jit_solution(9164687030123754085)
XLA Ops:
  0.6 165.9 %shard_map.85 = (bf16[4096,128]{1,0:T(8,128)(2,1)S(1)}, bf16[4096,128]{1,0:T(8,128)(2,1)S(1)}, bf16[4096,128]{1,0:T(8,128)(2,1)S(1)}) custom-call(bf16[4096,128]{1,0:T(8,128)(2,1)} %bitcast.8, bf16[4096,128]{1,0:T(8,128)(2,1)} %bitcast.9, bf16[4096,128]{1,0:T(8,128)(2,1)} %bitcast.10, bf16[4096,128]{1,0:T(8,128)(2,1)} %bitcast.11, ...), custom_call_target="tpu_custom_call" | custom-call | tf_op jit(solution)/shard_map/pallas_call | solution.py:308
  166.5 1.7 %shard_map.86 = (bf16[4096,128]{1,0:T(8,128)(2,1)}, bf16[4096,128]{1,0:T(8,128)(2,1)}, bf16[4096,128]{1,0:T(8,128)(2,1)}) custom-call(bf16[4096,128]{1,0:T(8,128)(2,1)S(1)} %get-tuple-element.9.dq_ref, bf16[4096,128]{1,0:T(8,128)(2,1)S(1)} %get-tuple-element.10.dk_ref, bf16[4096,128]{1,0:T(8,128)(2,1)S(1)} %get-tuple-element.11.dv_ref), custom_call_target="tpu_custom_call" | custom-call | tf_op jit(solution)/shard_map/pallas_call | solution.py:335

commit v4 on v3

--- a/solution.py
+++ b/solution.py
@@ -22,14 +22,14 @@
 TN = (((0,), (0,)), ((), ()))
 LOG2E = math.log2(math.e)
 U = 4
-GK = 2
+GK = 4
 GQ = 4
 SCALE = D ** -0.5
 
 
 def _kernel(k_hbm, v_hbm, q_hbm, do_hbm, o_hbm, lse_hbm, dq_out, dk_out, dv_out,
             xin, lsev, stage, ostage, statloc, buf, statbuf, rows, dq, dqin, dqs, kvs, rkv, rq, tmp, dk_acc, dv_acc,
-            s_in, r_in, s_fw, r_fw, s_kv, r_kv, s_x, r_x, s_q, r_q, s_st, r_st, s_ld):
+            s_in, r_in, s_fw, r_fw, s_kv, r_kv, s_x, r_x, s_q, r_q, s_st, r_st, s_ld, two, three):
     cp = lax.axis_index('cp')
     chip = cp // 2
     core = cp % 2
@@ -48,7 +48,7 @@
         x.start()
 
     def peer(i):
-        return lax.rem(chip + i, CH)
+        return lax.rem(chip + CH + jnp.where(chip < CH // 2, i, -i), CH)
 
     def dev(h):
         return {'cp': h * 2 + core}
@@ -70,23 +70,62 @@
         for h in range(CH):
             ostage[c, h] = tmp[4, pl.ds(h, R, stride=CH), :].astype(BF16)
 
+    def send_one(c, h):
+        rcopy(stage.at[c, h], buf.at[c, core, chip], s_in.at[c], r_in.at[c], dev(h)).start()
+
     def send(c):
-        for i in range(1, CH):
+        for i in range(CH - 1, 0, -1):
+            send_one(c, peer(i))
+
+    z = chip // 2
+    inner = z * (3 - z) // 2
+
+    def far(h):
+        return (h // 2 - z) * (h // 2 - z)
+
+    def send_at(c, dist):
+        for i in range(CH - 1, 0, -1):
             h = peer(i)
-            rcopy(stage.at[c, h], buf.at[c, core, chip], s_in.at[c], r_in.at[c], dev(h)).start()
+
+            @pl.when(far(h) <= 1 if dist == 1 else far(h) == dist * dist)
+            def _():
+                send_one(c, h)
+
+    def tell(sem, zz):
+        pl.semaphore_signal(sem, inc=1, device_id=dev(zz * 2 + chip % 2), device_id_type=MESH)
 
     def loop(lo, hi, f):
         lax.fori_loop(lo, hi, lambda x, _: (f(x), 0)[1], 0)
 
     barrier = pltpu.get_barrier_semaphore()
     pl.semaphore_signal(barrier, inc=1, device_id=sib, device_id_type=MESH)
-    for i in range(1, CH):
-        pl.semaphore_signal(barrier, inc=1, device_id=dev(peer(i)), device_id_type=MESH)
+    for i in range(CH - 1, 0, -1):
+        h = peer(i)
+
+        @pl.when(far(h) <= 1)
+        def _():
+            pl.semaphore_signal(barrier, inc=1, device_id=dev(h), device_id_type=MESH)
     for x in loads[:4]:
         x.wait()
     gather(C - 1)
-    pl.semaphore_wait(barrier, CH)
-    send(C - 1)
+    pl.semaphore_wait(barrier, 4 + 2 * inner)
+
+    @pl.when(inner == 1)
+    def _():
+        tell(two, 3 - z)
+        tell(two, 3 * (z - 1))
+    send_at(C - 1, 1)
+    pl.semaphore_wait(two, 1)
+
+    @pl.when(inner == 1)
+    def _():
+        tell(three, 3 * (z - 1))
+    send_at(C - 1, 2)
+
+    @pl.when(inner == 0)
+    def _():
+        pl.semaphore_wait(three, 1)
+    send_at(C - 1, 3)
     for x in loads[4:]:
         x.wait()
     gather(C - 2)
@@ -108,7 +147,7 @@
         statloc[h, :, :C * R] = lsev[h:h + 1, :]
         statloc[h, :, C * R:] = e[0:1, :]
     statbuf[core, chip] = statloc[chip]
-    for i in range(1, CH):
+    for i in range(CH - 1, 0, -1):
         h = peer(i)
         rcopy(statloc.at[h], statbuf.at[core, chip], s_st.at[0], r_st.at[0], dev(h)).start()
     loop(0, C - 4, lambda n: send(C - 5 - n))
@@ -177,7 +216,7 @@
                 dq[b, y] += part
 
     def send_kv(g):
-        for i in range(1, CH):
+        for i in range(CH - 1, 0, -1):
             h = peer(i)
             rcopy(kvs.at[g, h], rkv.at[g, chip], s_kv.at[g], r_kv.at[g], dev(h)).start()
 
@@ -216,7 +255,7 @@
         rq[g, chip, x] = dqs[g, chip, x]
 
     def send_q(g):
-        for i in range(1, CH):
+        for i in range(CH - 1, 0, -1):
             h = peer(i)
             rcopy(dqs.at[g, h], rq.at[g, chip], s_q.at[g], r_q.at[g], dev(h)).start()
 
@@ -328,7 +367,7 @@
                 pltpu.VMEM((5, KB, D), F32),
                 pltpu.VMEM((KB, D), F32),
                 pltpu.VMEM((KB, D), F32),
-            ] + [sem((C,))] * 10 + [sem((2,))] * 2 + [sem((2, 5))],
+            ] + [sem((C,))] * 10 + [sem((2,))] * 2 + [sem((2, 5))] + [pltpu.SemaphoreType.REGULAR] * 2,
             compiler_params=pltpu.CompilerParams(collective_id=0, has_side_effects=True,
                                                  vmem_limit_bytes=40 * 2 ** 20),
         )(*[pltpu.with_memory_space_constraint(x, pltpu.HBM) for x in (flat(k), flat(v), flat(q), flat(dout), flat(o), lse)])

time: 168 us -> 168 us (level)
  no operation moved by 1% of the time
where the time goes in v4:
time: 168 us; the launch traced here: 167 us
  Pallas kernels  167 us (99%)
    pallas_call x1, Pallas kernels, local(): pl.pallas_call(_kernel, out_shape=[pltpu.VMEM((c * h, d), BF16)] * 3, in_...  165 us

profile of v4, /device:TPU:0, one launch (start us, length us, event | category | flops | bytes accessed | tf_op | source)
XLA Modules:
  0.0 167.4 jit_solution(453625334313479465)
XLA Ops:
  0.6 165.1 %shard_map.85 = (bf16[4096,128]{1,0:T(8,128)(2,1)S(1)}, bf16[4096,128]{1,0:T(8,128)(2,1)S(1)}, bf16[4096,128]{1,0:T(8,128)(2,1)S(1)}) custom-call(bf16[4096,128]{1,0:T(8,128)(2,1)} %bitcast.8, bf16[4096,128]{1,0:T(8,128)(2,1)} %bitcast.9, bf16[4096,128]{1,0:T(8,128)(2,1)} %bitcast.10, bf16[4096,128]{1,0:T(8,128)(2,1)} %bitcast.11, ...), custom_call_target="tpu_custom_call" | custom-call | tf_op jit(solution)/shard_map/pallas_call | solution.py:347
  165.7 1.7 %shard_map.86 = (bf16[4096,128]{1,0:T(8,128)(2,1)}, bf16[4096,128]{1,0:T(8,128)(2,1)}, bf16[4096,128]{1,0:T(8,128)(2,1)}) custom-call(bf16[4096,128]{1,0:T(8,128)(2,1)S(1)} %get-tuple-element.9.dq_ref, bf16[4096,128]{1,0:T(8,128)(2,1)S(1)} %get-tuple-element.10.dk_ref, bf16[4096,128]{1,0:T(8,128)(2,1)S(1)} %get-tuple-element.11.dv_ref), custom_call_target="tpu_custom_call" | custom-call | tf_op jit(solution)/shard_map/pallas_call | solution.py:374

commit v5 on v4

--- a/solution.py
+++ b/solution.py
@@ -139,13 +139,13 @@
 
     ones = jnp.ones((8, D), BF16)
     for h in range(CH):
-        x = (stage[:, h, 3].astype(F32) * ostage[:, h].astype(F32)).reshape(C * R, D)
+        x = (stage[:, h, 3].astype(F32) * (ostage[:, h].astype(F32) * 0.5)).reshape(C * R, D)
         hi = x.astype(BF16)
         lo = (x - hi.astype(F32)).astype(BF16)
         e = (lax.dot_general(ones, hi, NT, preferred_element_type=F32)
              + lax.dot_general(ones, lo, NT, preferred_element_type=F32))
         statloc[h, :, :C * R] = lsev[h:h + 1, :]
-        statloc[h, :, C * R:] = e[0:1, :]
+        statloc[h, :, C * R:] = e[0:1, :] * 2.0
     statbuf[core, chip] = statloc[chip]
     for i in range(CH - 1, 0, -1):
         h = peer(i)
@@ -283,9 +283,9 @@
 
     loop(1, C // 2, last)
     make_kv(0)
-    send_kv(0)
     loop(C - 4, C, give_q)
     loop((C - 4) // GQ, C // GQ, send_q)
+    send_kv(0)
 
     def all_kv(g):
         return rcopy(kvs.at[g, pl.ds(0, CH - 1)], rkv.at[g, pl.ds(0, CH - 1)], s_kv.at[g], r_kv.at[g], sib)
@@ -302,7 +302,7 @@
                     tmp[t, pl.ds(h, R, stride=CH), :] = rkv[g, h, x, t].astype(F32)
                 ref[pl.ds(pl.multiple_of((g * GK + x) * KB, KB), KB), :] = tmp[t].astype(BF16)
 
-    loop(0, C // GK, put_kv)
+    loop(0, C // GK - 1, put_kv)
 
     def put_q(g):
         all_q(g).wait_recv()
@@ -321,6 +321,7 @@
     fst.wait_send()
     loop(0, C, drain)
     loop(0, C // GQ, put_q)
+    put_kv(C // GK - 1)
     loop(0, C // GK, lambda g: all_kv(g).wait_send())
     loop(0, C // GQ, lambda g: all_q(g).wait_send())
 

time: 168 us -> 167 us (level)
  Pallas kernels: 167 us -> 165 us
where the time goes in v5:
time: 167 us; the launch traced here: 166 us
  Pallas kernels  165 us (99%)
    pallas_call x1, Pallas kernels, local(): pl.pallas_call(_kernel, out_shape=[pltpu.VMEM((c * h, d), BF16)] * 3, in_...  164 us

profile of v5, /device:TPU:0, one launch (start us, length us, event | category | flops | bytes accessed | tf_op | source)
XLA Modules:
  0.0 165.9 jit_solution(17578665148468487888)
XLA Ops:
  0.6 163.6 %shard_map.85 = (bf16[4096,128]{1,0:T(8,128)(2,1)S(1)}, bf16[4096,128]{1,0:T(8,128)(2,1)S(1)}, bf16[4096,128]{1,0:T(8,128)(2,1)S(1)}) custom-call(bf16[4096,128]{1,0:T(8,128)(2,1)} %bitcast.8, bf16[4096,128]{1,0:T(8,128)(2,1)} %bitcast.9, bf16[4096,128]{1,0:T(8,128)(2,1)} %bitcast.10, bf16[4096,128]{1,0:T(8,128)(2,1)} %bitcast.11, ...), custom_call_target="tpu_custom_call" | custom-call | tf_op jit(solution)/shard_map/pallas_call | solution.py:348
  164.2 1.7 %shard_map.86 = (bf16[4096,128]{1,0:T(8,128)(2,1)}, bf16[4096,128]{1,0:T(8,128)(2,1)}, bf16[4096,128]{1,0:T(8,128)(2,1)}) custom-call(bf16[4096,128]{1,0:T(8,128)(2,1)S(1)} %get-tuple-element.9.dq_ref, bf16[4096,128]{1,0:T(8,128)(2,1)S(1)} %get-tuple-element.10.dk_ref, bf16[4096,128]{1,0:T(8,128)(2,1)S(1)} %get-tuple-element.11.dv_ref), custom_call_target="tpu_custom_call" | custom-call | tf_op jit(solution)/shard_map/pallas_call | solution.py:375

commit v6 on v5

--- a/solution.py
+++ b/solution.py
@@ -35,6 +35,18 @@
     core = cp % 2
     sib = {'cp': chip * 2 + 1 - core}
 
+    def peer(i):
+        return lax.rem(chip + CH + jnp.where(chip < CH // 2, i, -i), CH)
+
+    def dev(h):
+        return {'cp': h * 2 + core}
+
+    z = chip // 2
+    inner = z * (3 - z) // 2
+
+    def far(h):
+        return (h // 2 - z) * (h // 2 - z)
+
     hbm = (k_hbm, v_hbm, q_hbm, do_hbm, o_hbm)
     lead = (C - 1) * KB
     loads = []
@@ -44,14 +56,19 @@
         loads.append(pltpu.make_async_copy(hbm[t].at[pl.ds(0, lead)], xin.at[t, pl.ds(0, lead)], s_ld.at[1, t]))
     loads.append(pltpu.make_async_copy(o_hbm, xin.at[4], s_ld.at[0, 4]))
     loads.append(pltpu.make_async_copy(lse_hbm, lsev, s_ld.at[1, 4]))
-    for x in loads:
+    for x in loads[:4]:
         x.start()
-
-    def peer(i):
-        return lax.rem(chip + CH + jnp.where(chip < CH // 2, i, -i), CH)
-
-    def dev(h):
-        return {'cp': h * 2 + core}
+    barrier = pltpu.get_barrier_semaphore()
+    pl.semaphore_signal(barrier, inc=1, device_id=sib, device_id_type=MESH)
+    for i in range(CH - 1, 0, -1):
+        h = peer(i)
+
+        @pl.when(far(h) <= 1)
+        def _():
+            pl.semaphore_signal(barrier, inc=1, device_id=dev(h), device_id_type=MESH)
+    for x in loads[4:]:
+        x.start()
+
 
     def rcopy(src, dst, ss, rs, to):
         return pltpu.make_async_remote_copy(src_ref=src, dst_ref=dst, send_sem=ss, recv_sem=rs,
@@ -77,12 +94,6 @@
         for i in range(CH - 1, 0, -1):
             send_one(c, peer(i))
 
-    z = chip // 2
-    inner = z * (3 - z) // 2
-
-    def far(h):
-        return (h // 2 - z) * (h // 2 - z)
-
     def send_at(c, dist):
         for i in range(CH - 1, 0, -1):
             h = peer(i)
@@ -97,14 +108,6 @@
     def loop(lo, hi, f):
         lax.fori_loop(lo, hi, lambda x, _: (f(x), 0)[1], 0)
 
-    barrier = pltpu.get_barrier_semaphore()
-    pl.semaphore_signal(barrier, inc=1, device_id=sib, device_id_type=MESH)
-    for i in range(CH - 1, 0, -1):
-        h = peer(i)
-
-        @pl.when(far(h) <= 1)
-        def _():
-            pl.semaphore_signal(barrier, inc=1, device_id=dev(h), device_id_type=MESH)
     for x in loads[:4]:
         x.wait()
     gather(C - 1)
@@ -233,8 +236,8 @@
         clear()
         whole = n // U
         loop(0, whole, lambda u: [tile(c, c + 1 + U * u + x, False) for x in range(U)])
+        arrive(c - 1)
         loop(c + 1 + whole * U, C, lambda b: tile(c, b, False))
-        arrive(c - 1)
         tile(c, c, True)
         make_kv(c)
 

time: 167 us -> 167 us (level)
  no operation moved by 1% of the time
where the time goes in v6:
time: 167 us; the launch traced here: 166 us
  Pallas kernels  165 us (99%)
    pallas_call x1, Pallas kernels, local(): pl.pallas_call(_kernel, out_shape=[pltpu.VMEM((c * h, d), BF16)] * 3, in_...  164 us

profile of v6, /device:TPU:0, one launch (start us, length us, event | category | flops | bytes accessed | tf_op | source)
XLA Modules:
  0.0 166.0 jit_solution(17602595405482620781)
XLA Ops:
  0.6 163.6 %shard_map.85 = (bf16[4096,128]{1,0:T(8,128)(2,1)S(1)}, bf16[4096,128]{1,0:T(8,128)(2,1)S(1)}, bf16[4096,128]{1,0:T(8,128)(2,1)S(1)}) custom-call(bf16[4096,128]{1,0:T(8,128)(2,1)} %bitcast.8, bf16[4096,128]{1,0:T(8,128)(2,1)} %bitcast.9, bf16[4096,128]{1,0:T(8,128)(2,1)} %bitcast.10, bf16[4096,128]{1,0:T(8,128)(2,1)} %bitcast.11, ...), custom_call_target="tpu_custom_call" | custom-call | tf_op jit(solution)/shard_map/pallas_call | solution.py:351
  164.3 1.7 %shard_map.86 = (bf16[4096,128]{1,0:T(8,128)(2,1)}, bf16[4096,128]{1,0:T(8,128)(2,1)}, bf16[4096,128]{1,0:T(8,128)(2,1)}) custom-call(bf16[4096,128]{1,0:T(8,128)(2,1)S(1)} %get-tuple-element.9.dq_ref, bf16[4096,128]{1,0:T(8,128)(2,1)S(1)} %get-tuple-element.10.dk_ref, bf16[4096,128]{1,0:T(8,128)(2,1)S(1)} %get-tuple-element.11.dv_ref), custom_call_target="tpu_custom_call" | custom-call | tf_op jit(solution)/shard_map/pallas_call | solution.py:378
